TPU v7x, 32 devices: a whole 2x2x4 slice. The times are simulated.
32 devices in a mesh: box: 4 (over z), dir: 8 (over y, x, core).
Axes of the slice: x: 2, y: 2, z: 4, core: 2. Of those that a mesh axis runs over, the one named last changes fastest.
Arguments:
- currents: bfloat16 [4096, 256, 128], P(('box', 'dir')), may hold values from -6 to 6
- leaf_parent: int32 [4096], P(('box', 'dir')), may hold values from 0 to 63, as said below
- near_links: int32 [4096, 2], P(('box', 'dir')), may hold values 0 or 1
- near_blocks: bfloat16 [3, 256, 256], replicated, may hold values from -0.375 to 0.375
- aggregate_maps: bfloat16 [64, 256, 256], replicated, may hold values from -0.375 to 0.375
- far_boxes: int32 [64, 64], P('box'), may hold values from 0 to 63
- far_counts: int32 [64], P('box'), may hold values from 16 to 64
- translate_coef: float32 [64, 64, 256], P('box'), may hold values from 0.005 to 0.05
- time_kernel: float32 [128], replicated, may hold values from -0.5 to 0.5
- disaggregate_maps: bfloat16 [64, 256, 256], replicated, may hold values from -0.375 to 0.375
Outputs:
- field: bfloat16 [4096, 256, 128], P(('box', 'dir'))
Inputs may be any that keep to these rules, and one draw needn't show every extreme that they name: `leaf_parent`: the leaves k * 64 to (k + 1) * 64 - 1 share one parent. The leaves g * 1024 to (g + 1) * 1024 - 1 have as parents the top-level boxes g * 16 to (g + 1) * 16 - 1, each exactly once as a run.
All inputs are finite; a program needn't handle non-finite values. No bound on the sum of `near_links` on one device may be relied on, other than what follows from the above.
Results may differ from a plain program's by a relative error of at most 0.0047.
Values may be sent and summed in bfloat16 or wider, within the bound.
A program may use at most 192 MiB of HBM per device.

v0:
```python
import functools
import jax
import jax.numpy as jnp
from jax import lax
from jax.experimental import pallas as pl
from jax.experimental.pallas import tpu as pltpu
from jax.sharding import PartitionSpec as P

LEAF_TOP = 64
MESH = pl.DeviceIdType.MESH
HIGHEST = lax.Precision.HIGHEST


def aggregate_kernel(runs, chunk, maps_ref, cur_ref, out_ref, acc_ref):
    step = pl.program_id(0)
    samples = cur_ref.shape[-1]

    @pl.when(step == 0)
    def _():
        acc_ref[...] = jnp.zeros_like(acc_ref)

    total = acc_ref[...]
    for i in range(chunk):
        pair = jnp.concatenate([cur_ref[j, i] for j in range(runs)], axis=1)
        total = total + jnp.dot(maps_ref[i], pair, preferred_element_type=jnp.float32)
    acc_ref[...] = total

    @pl.when(step == pl.num_programs(0) - 1)
    def _():
        for j in range(runs):
            out_ref[j] = acc_ref[:, j * samples : (j + 1) * samples].astype(jnp.bfloat16)


def translate_kernel(
    boxes,
    dirs,
    runs,
    top_local,
    rays_ref,
    edge_ref,
    leaf_parent_ref,
    lists_ref,
    counts_ref,
    coef_ref,
    kernel_ref,
    out_ref,
    rim_ref,
    parent_ref,
    rim,
    rays_all,
    parent_all,
    weights_ref,
    far_ref,
    stage_ref,
    landed,
    ray_send,
    ray_recv,
    par_send,
    par_recv,
    back_send,
    back_recv,
    rim_send,
    rim_recv,
):
    my_box = lax.axis_index("box")
    my_dir = lax.axis_index("dir")
    me = my_box * dirs + my_dir
    devices = boxes * dirs
    rows = coef_ref.shape[2]
    samples = rays_ref.shape[-1]
    width = parent_ref.shape[-1]
    lane = lax.broadcasted_iota(jnp.int32, (1, width), 1)
    spare = jnp.where(me == 0, -1, 0)
    parent_row = jnp.where(lane >= devices * runs, spare, jnp.zeros((1, width), jnp.int32))
    for j in range(runs):
        parent_row = jnp.where(lane == me * runs + j, leaf_parent_ref[j * LEAF_TOP], parent_row)
    parent_ref[...] = parent_row.astype(jnp.float32)
    rim[...] = jnp.zeros_like(rim)
    peers = [(kb, kd) for kb in range(boxes) for kd in range(dirs) if kb or kd]
    peers.sort(key=lambda p: -min(p[0], boxes - p[0]))

    def target(kb, kd):
        return lax.rem(my_box + kb, boxes), lax.rem(my_dir + kd, dirs)

    barrier = pltpu.get_barrier_semaphore()
    for kb, kd in peers:
        tb, td = target(kb, kd)
        pl.semaphore_signal(
            barrier, inc=1, device_id={"box": tb, "dir": td}, device_id_type=MESH
        )
    pl.semaphore_wait(barrier, len(peers))

    def parent_copy(kb, kd):
        tb, td = target(kb, kd)
        return pltpu.make_async_remote_copy(
            src_ref=parent_ref,
            dst_ref=parent_all.at[me],
            send_sem=par_send.at[tb * dirs + td],
            recv_sem=par_recv.at[me],
            device_id={"box": tb, "dir": td},
            device_id_type=MESH,
        )

    def ray_copy(kb, kd):
        tb, td = target(kb, kd)
        block = pl.ds(pl.multiple_of(td * rows, rows), rows)
        return pltpu.make_async_remote_copy(
            src_ref=rays_ref.at[:, block, :],
            dst_ref=rays_all.at[me],
            send_sem=ray_send.at[tb * dirs + td],
            recv_sem=ray_recv.at[me],
            device_id={"box": tb, "dir": td},
            device_id_type=MESH,
        )

    def rim_copy(side):
        other = lax.rem(me + (1 if side == 0 else devices - 1), devices)
        return pltpu.make_async_remote_copy(
            src_ref=edge_ref.at[side],
            dst_ref=rim.at[side],
            send_sem=rim_send.at[side],
            recv_sem=rim_recv.at[side],
            device_id={"box": lax.div(other, dirs), "dir": lax.rem(other, dirs)},
            device_id_type=MESH,
        )

    for kb, kd in peers:
        parent_copy(kb, kd).start()
    for kb, kd in peers:
        ray_copy(kb, kd).start()

    @pl.when(me < devices - 1)
    def _():
        rim_copy(0).start()

    @pl.when(me > 0)
    def _():
        rim_copy(1).start()

    own = pl.ds(pl.multiple_of(my_dir * rows, rows), rows)
    rays_all[me] = rays_ref[:, own, :]
    parent_all[me] = parent_ref[...]

    lag = lax.broadcasted_iota(jnp.int32, (samples, samples), 1) - lax.broadcasted_iota(
        jnp.int32, (samples, samples), 0
    )

    def add_lag(i, matrix):
        return jnp.where(lag == i, kernel_ref[i], matrix)

    time_matrix = lax.fori_loop(
        0, samples, add_lag, jnp.zeros((samples, samples), jnp.float32)
    )

    def arrived(slot, buffer, sem):
        pltpu.make_async_remote_copy(
            src_ref=buffer.at[slot],
            dst_ref=buffer.at[slot],
            send_sem=sem.at[slot],
            recv_sem=sem.at[slot],
            device_id={"box": my_box, "dir": lax.rem(my_dir + 1, dirs)},
            device_id_type=MESH,
        ).wait_recv()

    for kb, kd in peers:
        sb, sd = target(kb, kd)
        arrived(sb * dirs + sd, parent_all, par_recv)
    parents = jnp.zeros((1, width), jnp.float32)
    for slot in range(devices):
        parents = parents + parent_all[slot]
    slots = lists_ref.shape[1]
    column = jnp.broadcast_to(parents, (128, width)).T[:, :slots]
    spot = lax.broadcasted_iota(jnp.int32, (1, slots), 1)
    for c in range(top_local):
        used = jnp.where(spot < counts_ref[c], lists_ref[c : c + 1, :], -2)
        match = (column == used.astype(jnp.float32)).astype(jnp.float32)
        weights_ref[c] = lax.dot_general(
            coef_ref[c],
            match,
            (((0,), (1,)), ((), ())),
            preferred_element_type=jnp.float32,
            precision=HIGHEST,
        )

    for kb, kd in peers:
        sb, sd = target(kb, kd)
        arrived(sb * dirs + sd, rays_all, ray_recv)

    group = 4 if top_local % 4 == 0 else 1

    def far_group(g, carry):
        base = g * group
        weight = [weights_ref[base + i] for i in range(group)]
        total = [jnp.zeros((rows, samples), jnp.float32) for _ in range(group)]
        for slot in range(boxes * dirs):
            for j in range(runs):
                ray = rays_all[slot, j].astype(jnp.float32)
                at = slot * runs + j
                for i in range(group):
                    total[i] = total[i] + weight[i][:, at : at + 1] * ray
        for i in range(group):
            far_ref[base + i] = total[i]
        return carry

    lax.fori_loop(0, top_local // group, far_group, 0)

    incoming = jnp.dot(
        far_ref[...].reshape(top_local * rows, samples),
        time_matrix,
        preferred_element_type=jnp.float32,
        precision=HIGHEST,
    )
    far_ref[...] = incoming.reshape(top_local, rows, samples)
    first_top = my_box * top_local
    for d in range(dirs):
        held = parent_all[my_box * dirs + d]
        for j in range(runs):
            at = (my_box * dirs + d) * runs + j
            parent = jnp.sum(jnp.where(lane == at, held, 0.0), axis=1, keepdims=True)
            chosen = jnp.zeros((rows, samples), jnp.float32)
            for c in range(top_local):
                hit = parent == (first_top + c).astype(jnp.float32)
                chosen = jnp.where(hit, far_ref[c], chosen)
            stage_ref[d, j] = chosen.astype(jnp.bfloat16)

    def back_copy(kd):
        td = lax.rem(my_dir + kd, dirs)
        return pltpu.make_async_remote_copy(
            src_ref=stage_ref.at[td],
            dst_ref=landed.at[my_dir],
            send_sem=back_send.at[td],
            recv_sem=back_recv.at[my_dir],
            device_id={"box": my_box, "dir": td},
            device_id_type=MESH,
        )

    for kd in range(1, dirs):
        back_copy(kd).start()
    landed[my_dir] = stage_ref[my_dir]
    for kb, kd in peers:
        parent_copy(kb, kd).wait_send()
        ray_copy(kb, kd).wait_send()

    @pl.when(me < devices - 1)
    def _():
        rim_copy(0).wait_send()
        rim_copy(1).wait_recv()

    @pl.when(me > 0)
    def _():
        rim_copy(1).wait_send()
        rim_copy(0).wait_recv()

    rim_ref[...] = rim[...]
    for kd in range(1, dirs):
        sd = lax.rem(my_dir + kd, dirs)
        arrived(sd, landed, back_recv)
    for d in range(dirs):
        for j in range(runs):
            out_ref[d * rows : (d + 1) * rows, j * samples : (j + 1) * samples] = landed[d, j]
    for kd in range(1, dirs):
        back_copy(kd).wait_send()


def field_kernel(
    runs, chunk, blocks_ref, maps_ref, incoming_ref, links_ref, cur_ref, rim_ref, out_ref
):
    step = pl.program_id(0)
    samples = cur_ref.shape[-1]
    first = step * chunk
    dot = functools.partial(jnp.dot, preferred_element_type=jnp.float32)

    def joined(parts):
        return jnp.concatenate(parts, axis=1)

    before = jnp.maximum(first - 1, 0)
    after = jnp.minimum(first + chunk, LEAF_TOP - 1)
    final = step == pl.num_programs(0) - 1
    lead = [rim_ref[0]] + [cur_ref[j, LEAF_TOP - 1] for j in range(runs - 1)]
    tail = [cur_ref[j, 0] for j in range(1, runs)] + [rim_ref[1]]
    lead = [jnp.where(step == 0, lead[j], cur_ref[j, before]) for j in range(runs)]
    tail = [jnp.where(final, tail[j], cur_ref[j, after]) for j in range(runs)]
    pairs = [joined(lead)]
    pairs += [joined([cur_ref[j, first + i] for j in range(runs)]) for i in range(chunk)]
    pairs += [joined(tail)]
    for i in range(chunk):
        at = first + i
        total = dot(blocks_ref[0], pairs[i + 1]) + dot(maps_ref[at], incoming_ref[...])
        low = dot(blocks_ref[1], pairs[i])
        high = dot(blocks_ref[2], pairs[i + 2])
        for j in range(runs):
            span = slice(j * samples, (j + 1) * samples)
            with_low = links_ref[0, j * LEAF_TOP + at].astype(jnp.float32)
            with_high = links_ref[1, j * LEAF_TOP + at].astype(jnp.float32)
            part = total[:, span] + with_low * low[:, span] + with_high * high[:, span]
            out_ref[j, i] = part.astype(jnp.bfloat16)


def per_device(
    currents,
    leaf_parent,
    near_links,
    near_blocks,
    aggregate_maps,
    far_boxes,
    far_counts,
    translate_coef,
    time_kernel,
    disaggregate_maps,
):
    boxes, dirs = lax.axis_size("box"), lax.axis_size("dir")
    devices = boxes * dirs
    leaf_count, unknowns, samples = currents.shape
    runs = leaf_count // LEAF_TOP
    top_local, list_slots = far_boxes.shape
    directions = aggregate_maps.shape[1]
    rows = directions // dirs
    dir_index = lax.axis_index("dir")
    f32, bf16 = jnp.float32, jnp.bfloat16

    leaf_runs = currents.reshape(runs, LEAF_TOP, unknowns, samples)

    chunk = 8
    steps = LEAF_TOP // chunk
    matmul_cost = 2 * leaf_count * samples * unknowns * directions
    vmem = pl.BlockSpec(memory_space=pltpu.VMEM)
    rays = pl.pallas_call(
        functools.partial(aggregate_kernel, runs, chunk),
        out_shape=jax.ShapeDtypeStruct((runs, directions, samples), bf16),
        grid=(steps,),
        in_specs=[
            pl.BlockSpec((chunk, directions, unknowns), lambda i: (i, 0, 0)),
            pl.BlockSpec((runs, chunk, unknowns, samples), lambda i: (0, i, 0, 0)),
        ],
        out_specs=pl.BlockSpec((runs, directions, samples), lambda i: (0, 0, 0)),
        scratch_shapes=[pltpu.VMEM((directions, runs * samples), f32)],
        cost_estimate=pl.CostEstimate(
            flops=matmul_cost, bytes_accessed=16 * 2**20, transcendentals=0
        ),
        name="aggregate",
    )(aggregate_maps, leaf_runs)

    total_runs = devices * runs
    width = -(-total_runs // 128) * 128
    coef = lax.dynamic_slice_in_dim(translate_coef, dir_index * rows, rows, 2)
    edges = jnp.stack([currents[-1], currents[0]])
    smem = pl.BlockSpec(memory_space=pltpu.SMEM)
    dma = pltpu.SemaphoreType.DMA
    incoming, rim = pl.pallas_call(
        functools.partial(translate_kernel, boxes, dirs, runs, top_local),
        out_shape=(
            jax.ShapeDtypeStruct((directions, runs * samples), bf16),
            jax.ShapeDtypeStruct((2, unknowns, samples), bf16),
        ),
        in_specs=[vmem, vmem, smem, vmem, smem, vmem, smem],
        out_specs=(vmem, vmem),
        scratch_shapes=[
            pltpu.VMEM((1, width), f32),
            pltpu.VMEM((2, unknowns, samples), bf16),
            pltpu.VMEM((devices, runs, rows, samples), bf16),
            pltpu.VMEM((devices, 1, width), f32),
            pltpu.VMEM((top_local, rows, width), f32),
            pltpu.VMEM((top_local, rows, samples), f32),
            pltpu.VMEM((dirs, runs, rows, samples), bf16),
            pltpu.VMEM((dirs, runs, rows, samples), bf16),
            dma((devices,)),
            dma((devices,)),
            dma((devices,)),
            dma((devices,)),
            dma((dirs,)),
            dma((dirs,)),
            dma((2,)),
            dma((2,)),
        ],
        compiler_params=pltpu.CompilerParams(
            collective_id=0, has_side_effects=True, vmem_limit_bytes=16 * 2**20
        ),
        cost_estimate=pl.CostEstimate(
            flops=8 * matmul_cost, bytes_accessed=2 * 2**20, transcendentals=0
        ),
        name="translate",
    )(rays, edges, leaf_parent, far_boxes, far_counts, coef, time_kernel)

    near_cost = 4 * matmul_cost
    out = pl.pallas_call(
        functools.partial(field_kernel, runs, chunk),
        out_shape=jax.ShapeDtypeStruct((runs, LEAF_TOP, unknowns, samples), bf16),
        grid=(steps,),
        in_specs=[vmem, vmem, vmem, smem, vmem, vmem],
        out_specs=pl.BlockSpec((runs, chunk, unknowns, samples), lambda i: (0, i, 0, 0)),
        cost_estimate=pl.CostEstimate(
            flops=near_cost, bytes_accessed=26 * 2**20, transcendentals=0
        ),
        name="field",
        compiler_params=pltpu.CompilerParams(vmem_limit_bytes=12 * 2**20),
    )(near_blocks, disaggregate_maps, incoming, near_links.T, leaf_runs, rim)
    return out.reshape(leaf_count, unknowns, samples)


def solution(mesh):
    return jax.shard_map(
        per_device,
        mesh=mesh,
        in_specs=(
            P(("box", "dir"), None, None),
            P(("box", "dir")),
            P(("box", "dir"), None),
            P(),
            P(),
            P("box", None),
            P("box"),
            P("box", None, None),
            P(),
            P(),
        ),
        out_specs=P(("box", "dir"), None, None),
        check_vma=False,
    )
```

profile of v0, /device:TPU:0, one launch (start us, length us, event | category | flops | bytes accessed | tf_op | source)
XLA Modules:
  0.0 53.3 jit_solution(12324544211489487901)
XLA Ops:
  0.0 0.0 copy-start
  0.0 0.0 copy-start.4
  0.0 0.0 copy-start.6
  0.0 0.0 copy-start.7
  0.0 0.0 copy-start.8
  0.0 9.8 %aggregate.1.rays_ref = bf16[2,256,128]{2,1,0:T(8,128)(2,1)} custom-call(bf16[64,256,256]{2,1,0:T(8,128)(2,1)} %maps_ref.2, bf16[2,64,256,128]{3,2,1,0:T(8,128)(2,1)} %bitcast.3), custom_call_target="tpu_custom_call" | custom-call | flops 2147483648 | bytes 16777216 | tf_op jit(solution)/shard_map/aggregate/pallas_call | solution.py:327
  9.8 0.9 %fusion = (bf16[1,256,128]{2,1,0:T(8,128)(2,1)S(1)}, bf16[1,256,128]{2,1,0:T(8,128)(2,1)S(1)}) fusion(bf16[128,256,128]{2,1,0:T(8,128)(2,1)} %param.10), kind=kLoop, calls=%fused_computation.2 | loop fusion | bytes 262144 | tf_op jit(solution)/shard_map/slice | solution.py:346
  10.7 0.0 copy-done
  10.8 0.0 slice-start
  10.8 0.2 constant_dynamic-slice_fusion.coef_ref
  11.0 0.0 copy-done.4
  11.0 0.0 copy-done.6
  11.0 0.0 copy-done.7
  11.0 0.0 copy-done.8
  11.0 0.0 copy-start.1
  11.0 1.0 %copy-done.1 = bf16[2,256,128]{2,1,0:T(8,128)(2,1)S(1)} copy-done((bf16[2,256,128]{2,1,0:T(8,128)(2,1)S(1)}, bf16[2,256,128]{2,1,0:T(8,128)(2,1)}, u32[]{:S(2)}) %copy-start.1) | copy-done | bytes 131096
  12.1 0.0 slice-start.1
  12.1 29.2 %translate.1 = (bf16[256,256]{1,0:T(8,128)(2,1)S(1)}, bf16[2,256,128]{2,1,0:T(8,128)(2,1)S(1)}) custom-call(bf16[2,256,128]{2,1,0:T(8,128)(2,1)S(1)} %copy-done.1, bf16[2,256,128]{2,1,0:T(8,128)(2,1)S(1)} %pad_maximum_fusion.edge_ref, s32[128]{0:T(128)S(1)} %copy-done.6, s32[16,64]{1,0:T(8,128)S(1)} %copy-done.4, s32[16]{0:T(128)S(1)} %copy-done.7, ...), custom_call_target="tpu_custom_call" | custom-call | flops 17179869184 | bytes 2097152 | tf_op jit(solution)/shard_map/translate/pallas_call | solution.py:349
  41.3 0.0 slice-done
  41.3 0.0 slice-done.1
  41.3 0.0 copy-done.2
  41.3 0.0 copy-done.3
  41.3 0.0 copy-done.5
  41.3 12.0 %field.1 = bf16[2,64,256,128]{3,2,1,0:T(8,128)(2,1)} custom-call(bf16[3,256,256]{2,1,0:T(8,128)(2,1)S(1)} %copy-done.3, bf16[64,256,256]{2,1,0:T(8,128)(2,1)S(1)} %copy-done.2, bf16[256,256]{1,0:T(8,128)(2,1)S(1)} %get-tuple-element.7.incoming_ref, s32[2,128]{1,0:T(2,128)S(1)} %bitcast.7, bf16[2,64,256,128]{3,2,1,0:T(8,128)(2,1)S(1)} %bitcast.6, ...), custom_call_target="tpu_custom_call" | custom-call | flops 8589934592 | bytes 27262976 | tf_op jit(solution)/shard_map/field/pallas_call | solution.py:385
  (5 shorter events, 0.0 us)
Async XLA Ops:
  0.0 10.8 %copy-start = (f32[16,64,256]{2,1,0:T(8,128)S(1)}, f32[16,64,256]{2,1,0:T(8,128)}, u32[]{:S(2)}) copy-start(f32[16,64,256]{2,1,0:T(8,128)} %param.17) | copy-start | bytes 3145732
  0.0 11.0 %copy-start.4 = (s32[16,64]{1,0:T(8,128)S(1)}, s32[16,64]{1,0:T(8,128)}, u32[]{:S(2)}) copy-start(s32[16,64]{1,0:T(8,128)} %lists_ref.1) | copy-start | bytes 12292
  0.0 11.0 %copy-start.6 = (s32[128]{0:T(128)S(1)}, s32[128]{0:T(128)}, u32[]{:S(2)}) copy-start(s32[128]{0:T(128)} %leaf_parent_ref.1) | copy-start | bytes 1540
  0.0 11.0 %copy-start.7 = (s32[16]{0:T(128)S(1)}, s32[16]{0:T(128)}, u32[]{:S(2)}) copy-start(s32[16]{0:T(128)} %counts_ref.1) | copy-start | bytes 196
  0.0 11.0 %copy-start.8 = (f32[128]{0:T(128)S(1)}, f32[128]{0:T(128)}, u32[]{:S(2)}) copy-start(f32[128]{0:T(128)} %kernel_ref.1) | copy-start | bytes 1540
  10.8 30.5 %slice-start = ((s8[8388608]{0:T(1024)(128)(4,1)}), s8[4194304]{0:T(1024)(128)(4,1)S(1)}, s32[]{:S(2)}) async-start(s8[8388608]{0:T(1024)(128)(4,1)} %bitcast.4), calls=%async_computation | async-start | bytes 8388608
  11.0 1.1 %copy-start.1 = (bf16[2,256,128]{2,1,0:T(8,128)(2,1)S(1)}, bf16[2,256,128]{2,1,0:T(8,128)(2,1)}, u32[]{:S(2)}) copy-start(bf16[2,256,128]{2,1,0:T(8,128)(2,1)} %aggregate.1.rays_ref) | copy-start | bytes 393220
  12.1 29.2 %slice-start.1 = ((s8[8388608]{0:T(1024)(128)(4,1)}), s8[4194304]{0:T(1024)(128)(4,1)S(1)}, s32[]{:S(2)}) async-start(s8[8388608]{0:T(1024)(128)(4,1)} %bitcast.4), calls=%async_computation.1 | async-start | bytes 8388608
  12.1 29.2 %copy-start.2 = (bf16[64,256,256]{2,1,0:T(8,128)(2,1)S(1)}, bf16[64,256,256]{2,1,0:T(8,128)(2,1)}, u32[]{:S(2)}) copy-start(bf16[64,256,256]{2,1,0:T(8,128)(2,1)} %maps_ref.3) | copy-start | bytes 25165828
  12.1 29.2 %copy-start.3 = (bf16[3,256,256]{2,1,0:T(8,128)(2,1)S(1)}, bf16[3,256,256]{2,1,0:T(8,128)(2,1)}, u32[]{:S(2)}) copy-start(bf16[3,256,256]{2,1,0:T(8,128)(2,1)} %blocks_ref.1) | copy-start | bytes 1179652
  12.1 29.2 %copy-start.5 = (s32[128,2]{0,1:T(2,128)S(1)}, s32[128,2]{0,1:T(2,128)}, u32[]{:S(2)}) copy-start(s32[128,2]{0,1:T(2,128)} %param.12) | copy-start | bytes 3076
where the time goes:
time: 54.1 us; the launch traced here: 53.3 us
  Pallas kernels  51 us (94%)
  local copies, waits for them, and re-layouts  2.18 us (4%)
    pallas_call x1, Pallas kernels, per_device(): pl.pallas_call(functools.partial(translate_kernel, boxes, dirs, runs, top...  29.2 us
    pallas_call x1, Pallas kernels, per_device(): pl.pallas_call(functools.partial(field_kernel, runs, chunk), out_shape=ja...  12 us
    pallas_call x1, Pallas kernels, per_device(): pl.pallas_call(functools.partial(aggregate_kernel, runs, chunk), out_shap...  9.82 us
    unnamed x22, local copies, waits for them, and re-layouts  1.09 us

commit v1 on v0

v1 whole, which is shorter than its diff:
```python
import functools
import jax
import jax.numpy as jnp
from jax import lax
from jax.experimental import pallas as pl
from jax.experimental.pallas import tpu as pltpu
from jax.sharding import PartitionSpec as P

MESH = pl.DeviceIdType.MESH
HIGHEST = lax.Precision.HIGHEST
F32 = jnp.float32
BF16 = jnp.bfloat16
AGG_CHUNK = 4
NEAR_UNROLL = 2


def split_high_low(value):
    high = value.astype(BF16)
    return high, (value - high.astype(F32)).astype(BF16)


def rays_kernel(
    boxes,
    dirs,
    runs,
    cur_hbm,
    agg_hbm,
    dis_hbm,
    coef_hbm,
    blocks_ref,
    links_ref,
    leaf_parent_ref,
    lists_ref,
    counts_ref,
    kernel_ref,
    incoming_ref,
    near_ref,
    dis_ref,
    leaf,
    acc,
    rays,
    rays_all,
    parent_row_ref,
    parent_all,
    coef,
    wide_ref,
    weights_ref,
    split_ref,
    spread_ref,
    far_ref,
    time_ref,
    stage_ref,
    landed,
    agg_sem,
    cur_sem,
    coef_sem,
    dis_sem,
    par_send,
    par_recv,
    ray_send,
    ray_recv,
    back_send,
    back_recv,
    rim_send,
    rim_recv,
):
    my_box = lax.axis_index("box")
    my_dir = lax.axis_index("dir")
    me = my_box * dirs + my_dir
    devices = boxes * dirs
    leaf_top = agg_hbm.shape[0]
    samples = cur_hbm.shape[-1]
    directions = agg_hbm.shape[1]
    rows = directions // dirs
    top_local = counts_ref.shape[0]
    slots = lists_ref.shape[1]
    width = parent_row_ref.shape[-1]
    places = dirs * runs
    plane = places * rows
    leaves = runs * leaf_top
    peers = [(kb, kd) for kb in range(boxes) for kd in range(dirs) if kb or kd]
    peers.sort(key=lambda p: -min(p[0], boxes - p[0]))

    def target(kb, kd):
        return lax.rem(my_box + kb, boxes), lax.rem(my_dir + kd, dirs)

    barrier = pltpu.get_barrier_semaphore()
    for kb, kd in peers:
        tb, td = target(kb, kd)
        pl.semaphore_signal(
            barrier, inc=1, device_id={"box": tb, "dir": td}, device_id_type=MESH
        )

    chunks = leaf_top // AGG_CHUNK

    def loads(c):
        first = c * AGG_CHUNK
        out = [
            pltpu.make_async_copy(
                agg_hbm.at[pl.ds(first, AGG_CHUNK)],
                dis_ref.at[pl.ds(first, AGG_CHUNK)],
                agg_sem.at[c],
            )
        ]
        for j in range(runs):
            at = j * leaf_top + first
            out.append(
                pltpu.make_async_copy(
                    cur_hbm.at[pl.ds(at, AGG_CHUNK)],
                    leaf.at[pl.ds(at + 1, AGG_CHUNK)],
                    cur_sem.at[j, c],
                )
            )
        return out

    def start_loads(c, carry):
        for copy in loads(c):
            copy.start()
        return carry

    lax.fori_loop(0, chunks, start_loads, 0)
    block_at = my_dir * rows
    lane_tile = lax.div(block_at, 128) * 128
    coef_copy = pltpu.make_async_copy(
        coef_hbm.at[:, :, pl.ds(pl.multiple_of(lane_tile, 128), 128)], coef, coef_sem
    )
    coef_copy.start()

    @pl.when(me == 0)
    def _():
        leaf[0] = jnp.zeros(leaf.shape[1:], BF16)

    @pl.when(me == devices - 1)
    def _():
        leaf[leaves + 1] = jnp.zeros(leaf.shape[1:], BF16)

    lane = lax.broadcasted_iota(jnp.int32, (1, width), 1)
    spare = jnp.where(me == 0, -1, 0)
    parent_row = jnp.where(lane >= devices * runs, spare, jnp.zeros((1, width), jnp.int32))
    for j in range(runs):
        parent_row = jnp.where(lane == me * runs + j, leaf_parent_ref[j * leaf_top], parent_row)
    parent_row_ref[...] = parent_row.astype(F32)
    acc[...] = jnp.zeros_like(acc)

    def aggregate(c, carry):
        for copy in loads(c):
            copy.wait()
        first = c * AGG_CHUNK
        maps = jnp.concatenate([dis_ref[first + i] for i in range(AGG_CHUNK)], axis=1)
        held = jnp.concatenate(
            [
                jnp.concatenate([leaf[1 + j * leaf_top + first + i] for j in range(runs)], axis=1)
                for i in range(AGG_CHUNK)
            ],
            axis=0,
        )
        acc[...] += jnp.dot(maps, held, preferred_element_type=F32)
        return carry

    lax.fori_loop(0, chunks // 2, aggregate, 0)

    pl.semaphore_wait(barrier, len(peers))

    def parent_copy(kb, kd):
        tb, td = target(kb, kd)
        return pltpu.make_async_remote_copy(
            src_ref=parent_row_ref,
            dst_ref=parent_all.at[me],
            send_sem=par_send.at[tb * dirs + td],
            recv_sem=par_recv.at[me],
            device_id={"box": tb, "dir": td},
            device_id_type=MESH,
        )

    def ray_copy(kb, kd):
        tb, td = target(kb, kd)
        block = pl.ds(pl.multiple_of(td * rows, rows), rows)
        return pltpu.make_async_remote_copy(
            src_ref=rays.at[:, block, :],
            dst_ref=rays_all.at[my_box, my_dir],
            send_sem=ray_send.at[tb * dirs + td],
            recv_sem=ray_recv.at[me],
            device_id={"box": tb, "dir": td},
            device_id_type=MESH,
        )

    def rim_copy(side):
        other = lax.rem(me + (1 if side == 0 else devices - 1), devices)
        return pltpu.make_async_remote_copy(
            src_ref=cur_hbm.at[leaves - 1 if side == 0 else 0],
            dst_ref=leaf.at[0 if side == 0 else leaves + 1],
            send_sem=rim_send.at[side],
            recv_sem=rim_recv.at[side],
            device_id={"box": lax.div(other, dirs), "dir": lax.rem(other, dirs)},
            device_id_type=MESH,
        )

    for kb, kd in peers:
        parent_copy(kb, kd).start()

    @pl.when(me < devices - 1)
    def _():
        rim_copy(0).start()

    @pl.when(me > 0)
    def _():
        rim_copy(1).start()

    parent_all[me] = parent_row_ref[...]

    lax.fori_loop(chunks // 2, chunks, aggregate, 0)

    for j in range(runs):
        rays[j] = acc[:, j * samples : (j + 1) * samples].astype(BF16)
    for kb, kd in peers:
        ray_copy(kb, kd).start()
    own = pl.ds(pl.multiple_of(block_at, rows), rows)
    rays_all[my_box, my_dir] = rays[:, own, :]
    dis_copy = pltpu.make_async_copy(dis_hbm, dis_ref, dis_sem)
    dis_copy.start()

    @pl.when(me < devices - 1)
    def _():
        rim_copy(0).wait_send()
        rim_copy(1).wait_recv()

    @pl.when(me > 0)
    def _():
        rim_copy(1).wait_send()
        rim_copy(0).wait_recv()

    def near_step(step, carry):
        blocks = jnp.concatenate([blocks_ref[k] for k in range(3)], axis=1)
        for u in range(NEAR_UNROLL):
            at = step * NEAR_UNROLL + u
            parts = [[], [], []]
            for j in range(runs):
                row = j * leaf_top + at
                low = leaf[row]
                high = leaf[row + 2]
                parts[0].append(leaf[row + 1])
                parts[1].append(jnp.where(links_ref[0, row] != 0, low, jnp.zeros_like(low)))
                parts[2].append(jnp.where(links_ref[1, row] != 0, high, jnp.zeros_like(high)))
            held = jnp.concatenate([jnp.concatenate(p, axis=1) for p in parts], axis=0)
            total = jnp.dot(blocks, held, preferred_element_type=F32)
            for j in range(runs):
                near_ref[j, at] = total[:, j * samples : (j + 1) * samples].astype(BF16)
        return carry

    lax.fori_loop(0, leaf_top // NEAR_UNROLL, near_step, 0)

    lag = lax.broadcasted_iota(jnp.int32, (samples, samples), 1) - lax.broadcasted_iota(
        jnp.int32, (samples, samples), 0
    )

    def add_lag(i, matrix):
        return jnp.where(lag == i, kernel_ref[i], matrix)

    time_matrix = lax.fori_loop(0, samples, add_lag, jnp.zeros((samples, samples), F32))
    time_high, time_low = split_high_low(time_matrix)
    time_ref[:samples, :samples] = time_high
    time_ref[:samples, samples:] = time_low
    time_ref[samples:, :samples] = time_high
    time_ref[samples:, samples:] = jnp.zeros_like(time_low)

    def arrived(ref, send_sem, recv_sem):
        pltpu.make_async_remote_copy(
            src_ref=ref,
            dst_ref=ref,
            send_sem=send_sem,
            recv_sem=recv_sem,
            device_id={"box": my_box, "dir": lax.rem(my_dir + 1, dirs)},
            device_id_type=MESH,
        ).wait_recv()

    for kb, kd in peers:
        sb, sd = target(kb, kd)
        slot = sb * dirs + sd
        arrived(parent_all.at[slot], par_send.at[slot], par_recv.at[slot])
    parents = jnp.zeros((1, width), F32)
    for slot in range(devices):
        parents = parents + parent_all[slot]
    column = jnp.broadcast_to(parents, (128, width)).T[:, :slots]
    spot = lax.broadcasted_iota(jnp.int32, (1, slots), 1)
    coef_copy.wait()
    inside = pl.ds(pl.multiple_of(block_at - lane_tile, rows), rows)
    for c in range(top_local):
        used = jnp.where(spot < counts_ref[c], lists_ref[c : c + 1, :], -2)
        match = (column == used.astype(F32)).astype(F32)
        wide_ref[c] = lax.dot_general(
            coef[c],
            match,
            (((0,), (1,)), ((), ())),
            preferred_element_type=F32,
            precision=HIGHEST,
        )
        weights_ref[c] = wide_ref[c, inside, :]
    first_top = my_box * top_local
    for place in range(places):
        at = my_box * places + place
        parent = jnp.sum(jnp.where(lane == at, parents, 0.0), axis=1, keepdims=True)
        chosen = jnp.zeros((rows, width), F32)
        for c in range(top_local):
            hit = parent == (first_top + c).astype(F32)
            chosen = jnp.where(hit, weights_ref[c], chosen)
        high, low = split_high_low(chosen)
        split_ref[place * rows : (place + 1) * rows, :] = high
        split_ref[plane + place * rows : plane + (place + 1) * rows, :] = low

    part = 256

    def spread(b, carry):
        for k in range(plane // part):
            spot_k = k * part + lax.broadcasted_iota(jnp.int32, (width, part), 1)
            owner = b * places + lax.div(spot_k, rows)
            pick = (owner == lax.broadcasted_iota(jnp.int32, (width, part), 0)).astype(F32)
            wide = jnp.dot(split_ref[...], pick.astype(BF16), preferred_element_type=F32)
            row_q = lax.rem(lax.broadcasted_iota(jnp.int32, (2 * plane, part), 0), rows)
            lane_q = lax.rem(lax.broadcasted_iota(jnp.int32, (2 * plane, part), 1), rows)
            spread_ref[b, :, k * part : (k + 1) * part] = jnp.where(
                row_q == lane_q, wide, 0.0
            ).astype(BF16)
        return carry

    lax.fori_loop(0, boxes, spread, 0)

    order = sorted(range(boxes), key=lambda kb: min(kb, boxes - kb))
    for n, kb in enumerate(order):
        sb = lax.rem(my_box + kb, boxes)
        for kd in range(dirs):
            if kb or kd:
                sd = lax.rem(my_dir + kd, dirs)
                slot = sb * dirs + sd
                arrived(rays_all.at[sb, sd], ray_send.at[slot], ray_recv.at[slot])
        held = rays_all[sb].reshape(plane, samples)
        part_sum = jnp.dot(spread_ref[sb], held, preferred_element_type=F32)
        if n == 0:
            far_ref[...] = part_sum
        else:
            far_ref[...] += part_sum

    far_high, far_low = split_high_low(far_ref[:plane, :] + far_ref[plane:, :])
    both = jnp.dot(
        jnp.concatenate([far_high, far_low], axis=1), time_ref[...], preferred_element_type=F32
    )
    incoming = (both[:, :samples] + both[:, samples:]).astype(BF16)
    for d in range(dirs):
        for j in range(runs):
            place = d * runs + j
            stage_ref[d, :, j * samples : (j + 1) * samples] = incoming[
                place * rows : (place + 1) * rows, :
            ]

    def back_copy(kd):
        td = lax.rem(my_dir + kd, dirs)
        return pltpu.make_async_remote_copy(
            src_ref=stage_ref.at[td],
            dst_ref=landed.at[my_dir],
            send_sem=back_send.at[td],
            recv_sem=back_recv.at[my_dir],
            device_id={"box": my_box, "dir": td},
            device_id_type=MESH,
        )

    for kd in range(1, dirs):
        back_copy(kd).start()
    landed[my_dir] = stage_ref[my_dir]
    for kb, kd in peers:
        parent_copy(kb, kd).wait_send()
        ray_copy(kb, kd).wait_send()
    dis_copy.wait()
    for kd in range(1, dirs):
        sd = lax.rem(my_dir + kd, dirs)
        arrived(landed.at[sd], back_send.at[sd], back_recv.at[sd])
    incoming_ref[...] = landed[...].reshape(directions, runs * samples)
    for kd in range(1, dirs):
        back_copy(kd).wait_send()


def field_kernel(runs, chunk, maps_ref, incoming_ref, near_ref, out_ref):
    first = pl.program_id(0) * chunk
    samples = near_ref.shape[-1]
    held = incoming_ref[...]
    for i in range(chunk):
        total = jnp.dot(maps_ref[first + i], held, preferred_element_type=F32)
        for j in range(runs):
            part = total[:, j * samples : (j + 1) * samples]
            out_ref[j, i] = (part + near_ref[j, first + i].astype(F32)).astype(BF16)


def per_device(
    currents,
    leaf_parent,
    near_links,
    near_blocks,
    aggregate_maps,
    far_boxes,
    far_counts,
    translate_coef,
    time_kernel,
    disaggregate_maps,
):
    boxes, dirs = lax.axis_size("box"), lax.axis_size("dir")
    devices = boxes * dirs
    leaf_count, unknowns, samples = currents.shape
    leaf_top, directions, _ = aggregate_maps.shape
    runs = leaf_count // leaf_top
    top_local, list_slots = far_boxes.shape
    rows = directions // dirs
    plane = top_local * rows
    chunks = leaf_top // AGG_CHUNK
    width = -(-devices * runs // 128) * 128

    held = functools.partial(pltpu.with_memory_space_constraint, memory_space=pltpu.HBM)
    hbm = pl.BlockSpec(memory_space=pltpu.HBM)
    vmem = pl.BlockSpec(memory_space=pltpu.VMEM)
    smem = pl.BlockSpec(memory_space=pltpu.SMEM)
    dma = pltpu.SemaphoreType.DMA
    incoming, near, maps = pl.pallas_call(
        functools.partial(rays_kernel, boxes, dirs, runs),
        out_shape=(
            jax.ShapeDtypeStruct((directions, runs * samples), BF16),
            jax.ShapeDtypeStruct((runs, leaf_top, unknowns, samples), BF16),
            jax.ShapeDtypeStruct(disaggregate_maps.shape, BF16),
        ),
        in_specs=[hbm, hbm, hbm, hbm, vmem, smem, smem, vmem, smem, smem],
        out_specs=(vmem, vmem, vmem),
        scratch_shapes=[
            pltpu.VMEM((leaf_count + 2, unknowns, samples), BF16),
            pltpu.VMEM((directions, runs * samples), F32),
            pltpu.VMEM((runs, directions, samples), BF16),
            pltpu.VMEM((boxes, dirs, runs, rows, samples), BF16),
            pltpu.VMEM((1, width), F32),
            pltpu.VMEM((devices, 1, width), F32),
            pltpu.VMEM((top_local, list_slots, 128), F32),
            pltpu.VMEM((top_local, 128, width), F32),
            pltpu.VMEM((top_local, rows, width), F32),
            pltpu.VMEM((2 * plane, width), BF16),
            pltpu.VMEM((boxes, 2 * plane, plane), BF16),
            pltpu.VMEM((2 * plane, samples), F32),
            pltpu.VMEM((2 * samples, 2 * samples), BF16),
            pltpu.VMEM((dirs, rows, runs * samples), BF16),
            pltpu.VMEM((dirs, rows, runs * samples), BF16),
            dma((chunks,)),
            dma((runs, chunks)),
            dma,
            dma,
            dma((devices,)),
            dma((devices,)),
            dma((devices,)),
            dma((devices,)),
            dma((dirs,)),
            dma((dirs,)),
            dma((2,)),
            dma((2,)),
        ],
        compiler_params=pltpu.CompilerParams(
            collective_id=0, has_side_effects=True, vmem_limit_bytes=30 * 2**20
        ),
        name="rays",
    )(
        held(currents),
        held(aggregate_maps),
        held(disaggregate_maps),
        held(translate_coef),
        held(near_blocks),
        held(near_links.T),
        held(leaf_parent),
        held(far_boxes),
        held(far_counts),
        held(time_kernel),
    )

    chunk = 8
    out = pl.pallas_call(
        functools.partial(field_kernel, runs, chunk),
        out_shape=jax.ShapeDtypeStruct((runs, leaf_top, unknowns, samples), BF16),
        grid=(leaf_top // chunk,),
        in_specs=[vmem, vmem, vmem],
        out_specs=pl.BlockSpec((runs, chunk, unknowns, samples), lambda i: (0, i, 0, 0)),
        name="field",
        compiler_params=pltpu.CompilerParams(vmem_limit_bytes=6 * 2**20),
    )(maps, incoming, near)
    return out.reshape(leaf_count, unknowns, samples)


def solution(mesh):
    return jax.shard_map(
        per_device,
        mesh=mesh,
        in_specs=(
            P(("box", "dir"), None, None),
            P(("box", "dir")),
            P(("box", "dir"), None),
            P(),
            P(),
            P("box", None),
            P("box"),
            P("box", None, None),
            P(),
            P(),
        ),
        out_specs=P(("box", "dir"), None, None),
        check_vma=False,
    )
```

time: 54.1 us -> 43.5 us (0.80); the launches traced: 53.3 us -> 43.3 us
  Pallas kernels: 51 us -> 43.3 us
  local copies, waits for them, and re-layouts: 2.18 us -> 0 us
    pallas_call x1, Pallas kernels: 12 us -> 6.11 us  [per_device(): pl.pallas_call(functools.partial(field_kernel, runs, chunk), out_shape=ja...]
    pallas_call x2 -> x1, Pallas kernels: 39 us -> 37.2 us  [per_device(): pl.pallas_call(functools.partial(rays_kernel, boxes, dirs, runs), out_sha...]
    unnamed x22 -> x0, local copies, waits for them, and re-layouts: 1.09 us -> none
    slice x1 -> x0, local copies, waits for them, and re-layouts: 0.88 us -> none  [per_device(): edges = jnp.stack([currents[-1], currents[0]])]
where the time goes in v1:
time: 43.5 us; the launch traced here: 43.3 us
  Pallas kernels  43.3 us (100%)
    pallas_call x1, Pallas kernels, per_device(): pl.pallas_call(functools.partial(rays_kernel, boxes, dirs, runs), out_sha...  37.2 us
    pallas_call x1, Pallas kernels, per_device(): pl.pallas_call(functools.partial(field_kernel, runs, chunk), out_shape=ja...  6.11 us

profile of v1, /device:TPU:0, one launch (start us, length us, event | category | flops | bytes accessed | tf_op | source)
XLA Modules:
  0.0 43.3 jit_solution(14820691220075574051)
XLA Ops:
  0.0 37.2 %rays.1 = (bf16[256,256]{1,0:T(8,128)(2,1)S(1)}, bf16[2,64,256,128]{3,2,1,0:T(8,128)(2,1)S(1)}, bf16[64,256,256]{2,1,0:T(8,128)(2,1)S(1)}) custom-call(bf16[128,256,128]{2,1,0:T(8,128)(2,1)} %cur_hbm.1, bf16[64,256,256]{2,1,0:T(8,128)(2,1)} %agg_hbm.1, bf16[64,256,256]{2,1,0:T(8,128)(2,1)} %dis_hbm.1, f32[16,64,256]{2,1,0:T(8,128)} %coef_hbm.1, ...), custom_call_target="tpu_custom_call" | custom-call | tf_op jit(solution)/shard_map/rays/pallas_call | solution.py:419
  37.2 6.1 %field.1 = bf16[2,64,256,128]{3,2,1,0:T(8,128)(2,1)} custom-call(bf16[64,256,256]{2,1,0:T(8,128)(2,1)S(1)} %get-tuple-element.8.maps_ref, bf16[256,256]{1,0:T(8,128)(2,1)S(1)} %get-tuple-element.9.incoming_ref, bf16[2,64,256,128]{3,2,1,0:T(8,128)(2,1)S(1)} %get-tuple-element.10.near_ref), custom_call_target="tpu_custom_call" | custom-call | tf_op jit(solution)/shard_map/field/pallas_call | solution.py:475

commit v2 on v1

v2 whole, which is shorter than its diff:
```python
import functools
import jax
import jax.numpy as jnp
from jax import lax
from jax.experimental import pallas as pl
from jax.experimental.pallas import tpu as pltpu
from jax.sharding import PartitionSpec as P

MESH = pl.DeviceIdType.MESH
F32 = jnp.float32
BF16 = jnp.bfloat16
AGG_CHUNK = 4
NEAR_BLOCK = 8
REACH = 2
RELAY_FROM = 2


def split_high_low(value):
    high = value.astype(BF16)
    return high, (value - high.astype(F32)).astype(BF16)


def rays_kernel(
    boxes,
    dirs,
    runs,
    cur_hbm,
    agg_hbm,
    dis_hbm,
    coef_hbm,
    blocks_hbm,
    links_hbm,
    leaf_parent_hbm,
    lists_hbm,
    counts_hbm,
    kernel_hbm,
    incoming_ref,
    near_ref,
    dis_ref,
    leaf,
    acc,
    rays,
    rays_all,
    blocks_ref,
    links_ref,
    leaf_parent_ref,
    lists_ref,
    counts_ref,
    kernel_ref,
    parent_row_ref,
    parent_all,
    coef,
    weights_ref,
    split_ref,
    spread_ref,
    far_ref,
    time_ref,
    stage_ref,
    landed,
    agg_sem,
    cur_sem,
    small_sem,
    dis_sem,
    par_send,
    par_recv,
    ray_send,
    ray_recv,
    relay_send,
    back_send,
    back_recv,
    rim_send,
    rim_recv,
):
    my_box = lax.axis_index("box")
    my_dir = lax.axis_index("dir")
    me = my_box * dirs + my_dir
    devices = boxes * dirs
    leaf_top = agg_hbm.shape[0]
    samples = cur_hbm.shape[-1]
    directions = agg_hbm.shape[1]
    rows = directions // dirs
    top_local = counts_ref.shape[0]
    slots = lists_ref.shape[1]
    width = parent_row_ref.shape[-1]
    places = dirs * runs
    group = far_ref.shape[1] // 2
    cut = group // places
    leaves = runs * leaf_top
    dot = functools.partial(jnp.dot, preferred_element_type=F32)
    peers = [(kb, kd) for kb in range(boxes) for kd in range(dirs) if kb or kd]

    def target(kb, kd):
        return lax.rem(my_box + kb, boxes), lax.rem(my_dir + kd, dirs)

    chunks = leaf_top // AGG_CHUNK

    def loads(c):
        first = c * AGG_CHUNK
        out = []
        for j in range(runs):
            at = j * leaf_top + first
            out.append(
                pltpu.make_async_copy(
                    cur_hbm.at[pl.ds(at, AGG_CHUNK)],
                    leaf.at[pl.ds(at + 1, AGG_CHUNK)],
                    cur_sem.at[j, c],
                )
            )
        out.append(
            pltpu.make_async_copy(
                agg_hbm.at[pl.ds(first, AGG_CHUNK)],
                dis_ref.at[pl.ds(first, AGG_CHUNK)],
                agg_sem.at[c],
            )
        )
        return out

    def start_loads(c, carry):
        for copy in loads(c):
            copy.start()
        return carry

    block_at = my_dir * rows
    lane_tile = lax.div(block_at, 128) * 128
    small = [
        (leaf_parent_hbm, leaf_parent_ref),
        (links_hbm, links_ref),
        (counts_hbm, counts_ref),
        (kernel_hbm, kernel_ref),
        (lists_hbm, lists_ref),
        (blocks_hbm, blocks_ref),
        (coef_hbm.at[:, :, pl.ds(pl.multiple_of(lane_tile, 128), 128)], coef),
    ]
    small = [pltpu.make_async_copy(a, b, small_sem.at[i]) for i, (a, b) in enumerate(small)]
    small[0].start()
    lax.fori_loop(0, chunks, start_loads, 0)
    for copy in small[1:]:
        copy.start()

    barrier = pltpu.get_barrier_semaphore()
    for kb, kd in peers:
        tb, td = target(kb, kd)
        pl.semaphore_signal(
            barrier, inc=1, device_id={"box": tb, "dir": td}, device_id_type=MESH
        )

    @pl.when(me == 0)
    def _():
        leaf[0] = jnp.zeros(leaf.shape[1:], BF16)

    @pl.when(me == devices - 1)
    def _():
        leaf[leaves + 1] = jnp.zeros(leaf.shape[1:], BF16)

    small[0].wait()
    lane = lax.broadcasted_iota(jnp.int32, (1, width), 1)
    spare = jnp.where(me == 0, -1, 0)
    parent_row = jnp.where(lane >= devices * runs, spare, jnp.zeros((1, width), jnp.int32))
    for j in range(runs):
        parent_row = jnp.where(lane == me * runs + j, leaf_parent_ref[j * leaf_top], parent_row)
    parent_row_ref[...] = parent_row.astype(F32)
    parent_all[me] = parent_row.astype(F32)
    acc[...] = jnp.zeros_like(acc)

    def aggregate(c, carry):
        for copy in loads(c):
            copy.wait()
        first = c * AGG_CHUNK
        maps = jnp.concatenate([dis_ref[first + i] for i in range(AGG_CHUNK)], axis=1)
        held = jnp.concatenate(
            [
                jnp.concatenate([leaf[1 + j * leaf_top + first + i] for j in range(runs)], axis=1)
                for i in range(AGG_CHUNK)
            ],
            axis=0,
        )
        acc[...] += dot(maps, held)
        return carry

    lax.fori_loop(0, chunks, aggregate, 0)

    def parent_copy(kb, kd):
        tb, td = target(kb, kd)
        return pltpu.make_async_remote_copy(
            src_ref=parent_row_ref,
            dst_ref=parent_all.at[me],
            send_sem=par_send.at[tb * dirs + td],
            recv_sem=par_recv.at[me],
            device_id={"box": tb, "dir": td},
            device_id_type=MESH,
        )

    def ray_copy(delta, kd):
        tb = my_box + delta
        td = lax.rem(my_dir + kd, dirs)
        block = pl.ds(pl.multiple_of(td * rows, rows), rows)
        return pltpu.make_async_remote_copy(
            src_ref=rays.at[:, block, :],
            dst_ref=rays_all.at[my_box, my_dir],
            send_sem=ray_send.at[(delta + REACH) * dirs + td],
            recv_sem=ray_recv.at[me],
            device_id={"box": tb, "dir": td},
            device_id_type=MESH,
        )

    def relay_copy(side, away, sd):
        sb = my_box - side * away
        slot = sb * dirs + sd
        return pltpu.make_async_remote_copy(
            src_ref=rays_all.at[sb, sd],
            dst_ref=rays_all.at[sb, sd],
            send_sem=relay_send.at[slot],
            recv_sem=ray_recv.at[slot],
            device_id={"box": my_box + side, "dir": my_dir},
            device_id_type=MESH,
        )

    def rim_copy(side):
        other = lax.rem(me + (1 if side == 0 else devices - 1), devices)
        return pltpu.make_async_remote_copy(
            src_ref=cur_hbm.at[leaves - 1 if side == 0 else 0],
            dst_ref=leaf.at[0 if side == 0 else leaves + 1],
            send_sem=rim_send.at[side],
            recv_sem=rim_recv.at[side],
            device_id={"box": lax.div(other, dirs), "dir": lax.rem(other, dirs)},
            device_id_type=MESH,
        )

    def inside(box):
        return jnp.logical_and(box >= 0, box < boxes)

    def when_sending(delta, action):
        def every():
            for kd in range(dirs):
                if delta or kd:
                    action(ray_copy(delta, kd))

        if delta:
            pl.when(inside(my_box + delta))(every)
        else:
            every()

    for j in range(runs):
        rays[j] = acc[:, j * samples : (j + 1) * samples].astype(BF16)
    pl.semaphore_wait(barrier, len(peers))
    deltas = sorted(range(-REACH, REACH + 1), key=lambda delta: -abs(delta))
    deltas = [delta for delta in deltas if abs(delta) < boxes]
    for delta in deltas:
        when_sending(delta, lambda copy: copy.start())
    for kb, kd in peers:
        parent_copy(kb, kd).start()

    @pl.when(me < devices - 1)
    def _():
        rim_copy(0).start()

    @pl.when(me > 0)
    def _():
        rim_copy(1).start()

    own = pl.ds(pl.multiple_of(block_at, rows), rows)
    rays_all[my_box, my_dir] = rays[:, own, :]
    dis_copy = pltpu.make_async_copy(dis_hbm, dis_ref, dis_sem)
    dis_copy.start()
    for copy in small[1:]:
        copy.wait()

    def near_block(step):
        first = step * NEAR_BLOCK
        pairs = [
            jnp.concatenate([leaf[j * leaf_top + first + u] for j in range(runs)], axis=1)
            for u in range(NEAR_BLOCK + 2)
        ]
        for u in range(NEAR_BLOCK):
            mid = dot(blocks_ref[0], pairs[u + 1])
            low = dot(blocks_ref[1], pairs[u])
            high = dot(blocks_ref[2], pairs[u + 2])
            for j in range(runs):
                span = slice(j * samples, (j + 1) * samples)
                at = j * leaf_top + first + u
                with_low = links_ref[0, at].astype(F32)
                with_high = links_ref[1, at].astype(F32)
                part = mid[:, span] + with_low * low[:, span] + with_high * high[:, span]
                near_ref[j, first + u] = part.astype(BF16)

    def arrived(ref, send_sem, recv_sem):
        pltpu.make_async_remote_copy(
            src_ref=ref,
            dst_ref=ref,
            send_sem=send_sem,
            recv_sem=recv_sem,
            device_id={"box": my_box, "dir": lax.rem(my_dir + 1, dirs)},
            device_id_type=MESH,
        ).wait_recv()

    def ray_arrived(sb, sd):
        slot = sb * dirs + sd
        arrived(rays_all.at[sb, sd], relay_send.at[slot], ray_recv.at[slot])

    def each_relay(action):
        for away in range(REACH, boxes - 1):
            for side in (1, -1):
                fits = jnp.logical_and(inside(my_box - side * away), inside(my_box + side))
                pl.when(fits)(functools.partial(action, side, away))

    blocks = leaf_top // NEAR_BLOCK
    per_step = -(-dirs // (blocks - 2 - RELAY_FROM))

    def near_step(step, carry):
        near_block(step + 1)

        @pl.when(step >= RELAY_FROM)
        def _():
            def forward(side, away):
                for i in range(per_step):
                    sd = (step - RELAY_FROM) * per_step + i

                    @pl.when(sd < dirs)
                    def _():
                        ray_arrived(my_box - side * away, sd)
                        relay_copy(side, away, sd).start()

            each_relay(forward)

        return carry

    lax.fori_loop(0, blocks - 2, near_step, 0)

    spread_time = pltpu.roll(
        jnp.broadcast_to(kernel_ref[...], (samples, samples)), 0, 1, stride=1, stride_axis=0
    )
    causal = lax.broadcasted_iota(jnp.int32, (samples, samples), 1) >= lax.broadcasted_iota(
        jnp.int32, (samples, samples), 0
    )
    time_high, time_low = split_high_low(jnp.where(causal, spread_time, 0.0))
    time_ref[:samples, :samples] = time_high
    time_ref[:samples, samples:] = time_low
    time_ref[samples:, :samples] = time_high
    time_ref[samples:, samples:] = jnp.zeros_like(time_low)

    for kb, kd in peers:
        sb, sd = target(kb, kd)
        slot = sb * dirs + sd
        arrived(parent_all.at[slot], par_send.at[slot], par_recv.at[slot])
    parents = jnp.zeros((1, width), F32)
    for slot in range(devices):
        parents = parents + parent_all[slot]
    column = jnp.broadcast_to(parents, (128, width)).T[:, :slots]
    spot = lax.broadcasted_iota(jnp.int32, (1, slots), 1)
    turn = lax.rem(128 - (block_at - lane_tile), 128)
    for c in range(top_local):
        used = jnp.where(spot < counts_ref[c], lists_ref[c : c + 1, :], -2)
        match = (column == used.astype(F32)).astype(F32).astype(BF16)
        high, low = split_high_low(pltpu.roll(coef[c], turn, 1)[:, :rows])
        both = lax.dot_general(
            jnp.concatenate([high, low], axis=1),
            match,
            (((0,), (1,)), ((), ())),
            preferred_element_type=F32,
        )
        high, low = split_high_low(both[:rows, :] + both[rows:, :])
        weights_ref[c * rows : (c + 1) * rows, :width] = high
        weights_ref[c * rows : (c + 1) * rows, width:] = low

    def iota(shape, axis):
        return lax.broadcasted_iota(jnp.int32, shape, axis)

    total = places * rows
    for g in range(total // group):
        place = lax.div(iota((group, width), 0), cut)
        here = iota((group, width), 1) == my_box * places + place
        parent = jnp.sum(jnp.where(here, parents, 0.0), axis=1, keepdims=True)
        shape = (group, total)
        owner = (my_box * top_local + lax.div(iota(shape, 1), rows)).astype(F32)
        same = lax.rem(iota(shape, 1), rows) == g * cut + lax.rem(iota(shape, 0), cut)
        pick = jnp.where(jnp.logical_and(parent == owner, same), 1.0, 0.0).astype(BF16)
        moved = dot(pick, weights_ref[...]).astype(BF16)
        split_ref[g, :group, :] = moved[:, :width]
        split_ref[g, group:, :] = moved[:, width:]

    def spread(b, carry):
        shape = (width, group)
        pick = iota(shape, 0) == b * places + lax.div(iota(shape, 1), cut)
        pick = jnp.where(pick, 1.0, 0.0).astype(BF16)
        shape = (2 * group, group)
        same = lax.rem(iota(shape, 0), cut) == lax.rem(iota(shape, 1), cut)
        for g in range(total // group):
            spread_ref[b, g] = jnp.where(same, dot(split_ref[g], pick), 0.0).astype(BF16)
        return carry

    lax.fori_loop(0, boxes, spread, 0)

    half = lax.div(my_box * 2, boxes)
    for n in range(boxes):
        sb = lax.rem(my_box + n * (1 - 2 * half) + boxes, boxes)

        def plain():
            for kd in range(1 if n == 0 else 0, dirs):
                ray_arrived(sb, lax.rem(my_dir + kd, dirs))

        if n == 0:
            plain()
        else:
            up = jnp.logical_and(sb <= my_box - REACH, my_box + 1 < boxes)
            down = jnp.logical_and(sb >= my_box + REACH, my_box >= 1)
            pl.when(jnp.logical_not(jnp.logical_or(up, down)))(plain)
        for g in range(total // group):
            held = rays_all[sb, :, :, g * cut : (g + 1) * cut, :].reshape(group, samples)
            part_sum = dot(spread_ref[sb, g], held)
            if n == 0:
                far_ref[g] = part_sum
            else:
                far_ref[g] += part_sum

    for g in range(total // group):
        high, low = split_high_low(far_ref[g, :group, :] + far_ref[g, group:, :])
        both = dot(jnp.concatenate([high, low], axis=1), time_ref[...])
        incoming = (both[:, :samples] + both[:, samples:]).astype(BF16)
        for d in range(dirs):
            for j in range(runs):
                place = d * runs + j
                stage_ref[d, g * cut : (g + 1) * cut, j * samples : (j + 1) * samples] = incoming[
                    place * cut : (place + 1) * cut, :
                ]

    def back_copy(kd):
        td = lax.rem(my_dir + kd, dirs)
        return pltpu.make_async_remote_copy(
            src_ref=stage_ref.at[td],
            dst_ref=landed.at[my_dir],
            send_sem=back_send.at[td],
            recv_sem=back_recv.at[my_dir],
            device_id={"box": my_box, "dir": td},
            device_id_type=MESH,
        )

    for kd in range(1, dirs):
        back_copy(kd).start()
    landed[my_dir] = stage_ref[my_dir]

    @pl.when(me < devices - 1)
    def _():
        rim_copy(0).wait_send()
        rim_copy(1).wait_recv()

    @pl.when(me > 0)
    def _():
        rim_copy(1).wait_send()
        rim_copy(0).wait_recv()

    def last_block(step, carry):
        near_block(step * (blocks - 1))
        return carry

    lax.fori_loop(0, 2, last_block, 0)
    for kb, kd in peers:
        parent_copy(kb, kd).wait_send()
    for delta in deltas:
        when_sending(delta, lambda copy: copy.wait_send())

    def relayed(side, away):
        for sd in range(dirs):
            relay_copy(side, away, sd).wait_send()

    each_relay(relayed)
    dis_copy.wait()
    for kd in range(1, dirs):
        sd = lax.rem(my_dir + kd, dirs)
        arrived(landed.at[sd], back_send.at[sd], back_recv.at[sd])
    incoming_ref[...] = landed[...].reshape(directions, runs * samples)
    for kd in range(1, dirs):
        back_copy(kd).wait_send()


def field_kernel(runs, chunk, maps_ref, incoming_ref, near_ref, out_ref, held_out, sem):
    leaf_top, _, _ = maps_ref.shape
    samples = near_ref.shape[-1]
    held = incoming_ref[...]

    def copy(step):
        span = pl.ds(step * chunk, chunk)
        return pltpu.make_async_copy(held_out.at[:, span], out_ref.at[:, span], sem.at[step])

    def step_of(step, carry):
        for i in range(chunk):
            at = step * chunk + i
            total = jnp.dot(maps_ref[at], held, preferred_element_type=F32)
            for j in range(runs):
                part = total[:, j * samples : (j + 1) * samples]
                held_out[j, at] = (part + near_ref[j, at].astype(F32)).astype(BF16)
        copy(step).start()
        return carry

    def finish(step, carry):
        copy(step).wait()
        return carry

    steps = leaf_top // chunk
    lax.fori_loop(0, steps, step_of, 0, unroll=4)
    lax.fori_loop(0, steps, finish, 0)


def per_device(
    currents,
    leaf_parent,
    near_links,
    near_blocks,
    aggregate_maps,
    far_boxes,
    far_counts,
    translate_coef,
    time_kernel,
    disaggregate_maps,
):
    boxes, dirs = lax.axis_size("box"), lax.axis_size("dir")
    devices = boxes * dirs
    leaf_count, unknowns, samples = currents.shape
    leaf_top, directions, _ = aggregate_maps.shape
    runs = leaf_count // leaf_top
    top_local, list_slots = far_boxes.shape
    rows = directions // dirs
    plane = top_local * rows
    cut = min(rows, 16)
    group = top_local * cut
    groups = rows // cut
    chunks = leaf_top // AGG_CHUNK
    width = -(-devices * runs // 128) * 128

    held = functools.partial(pltpu.with_memory_space_constraint, memory_space=pltpu.HBM)
    hbm = pl.BlockSpec(memory_space=pltpu.HBM)
    vmem = pl.BlockSpec(memory_space=pltpu.VMEM)
    smem = pl.BlockSpec(memory_space=pltpu.SMEM)
    dma = pltpu.SemaphoreType.DMA
    incoming, near, maps = pl.pallas_call(
        functools.partial(rays_kernel, boxes, dirs, runs),
        out_shape=(
            jax.ShapeDtypeStruct((directions, runs * samples), BF16),
            jax.ShapeDtypeStruct((runs, leaf_top, unknowns, samples), BF16),
            jax.ShapeDtypeStruct(disaggregate_maps.shape, BF16),
        ),
        in_specs=[hbm] * 10,
        out_specs=(vmem, vmem, vmem),
        scratch_shapes=[
            pltpu.VMEM((leaf_count + 2, unknowns, samples), BF16),
            pltpu.VMEM((directions, runs * samples), F32),
            pltpu.VMEM((runs, directions, samples), BF16),
            pltpu.VMEM((boxes, dirs, runs, rows, samples), BF16),
            pltpu.VMEM(near_blocks.shape, BF16),
            pltpu.SMEM((2, leaf_count), jnp.int32),
            pltpu.SMEM((leaf_count,), jnp.int32),
            pltpu.VMEM((top_local, list_slots), jnp.int32),
            pltpu.SMEM((top_local,), jnp.int32),
            pltpu.VMEM((1, samples), F32),
            pltpu.VMEM((1, width), F32),
            pltpu.VMEM((devices, 1, width), F32),
            pltpu.VMEM((top_local, list_slots, 128), F32),
            pltpu.VMEM((plane, 2 * width), BF16),
            pltpu.VMEM((groups, 2 * group, width), BF16),
            pltpu.VMEM((boxes, groups, 2 * group, group), BF16),
            pltpu.VMEM((groups, 2 * group, samples), F32),
            pltpu.VMEM((2 * samples, 2 * samples), BF16),
            pltpu.VMEM((dirs, rows, runs * samples), BF16),
            pltpu.VMEM((dirs, rows, runs * samples), BF16),
            dma((chunks,)),
            dma((runs, chunks)),
            dma((7,)),
            dma,
            dma((devices,)),
            dma((devices,)),
            dma(((2 * REACH + 1) * dirs,)),
            dma((devices,)),
            dma((devices,)),
            dma((dirs,)),
            dma((dirs,)),
            dma((2,)),
            dma((2,)),
        ],
        compiler_params=pltpu.CompilerParams(
            collective_id=0, has_side_effects=True, vmem_limit_bytes=30 * 2**20
        ),
        name="rays",
    )(
        held(currents),
        held(aggregate_maps),
        held(disaggregate_maps),
        held(translate_coef),
        held(near_blocks),
        held(near_links.T),
        held(leaf_parent),
        held(far_boxes),
        held(far_counts),
        held(time_kernel.reshape(1, samples)),
    )

    chunk = 4
    out_shape = (runs, leaf_top, unknowns, samples)
    out = pl.pallas_call(
        functools.partial(field_kernel, runs, chunk),
        out_shape=jax.ShapeDtypeStruct(out_shape, BF16),
        in_specs=[vmem, vmem, vmem],
        out_specs=hbm,
        scratch_shapes=[pltpu.VMEM(out_shape, BF16), dma((leaf_top // chunk,))],
        name="field",
        compiler_params=pltpu.CompilerParams(vmem_limit_bytes=10 * 2**20),
    )(maps, incoming, near)
    return out.reshape(leaf_count, unknowns, samples)


def solution(mesh):
    return jax.shard_map(
        per_device,
        mesh=mesh,
        in_specs=(
            P(("box", "dir"), None, None),
            P(("box", "dir")),
            P(("box", "dir"), None),
            P(),
            P(),
            P("box", None),
            P("box"),
            P("box", None, None),
            P(),
            P(),
        ),
        out_specs=P(("box", "dir"), None, None),
        check_vma=False,
    )
```

time: 43.5 us -> 33.9 us (0.78)
  Pallas kernels: 43.3 us -> 33.7 us
    pallas_call x1, Pallas kernels: 37.2 us -> 29.8 us  [per_device(): pl.pallas_call(functools.partial(rays_kernel, boxes, dirs, runs), out_sha...]
    pallas_call x1, Pallas kernels: 6.11 us -> 3.89 us  [per_device(): pl.pallas_call(functools.partial(field_kernel, runs, chunk), out_shape=ja...]
where the time goes in v2:
time: 33.9 us; the launch traced here: 33.7 us
  Pallas kernels  33.7 us (99%)
    pallas_call x1, Pallas kernels, per_device(): pl.pallas_call(functools.partial(rays_kernel, boxes, dirs, runs), out_sha...  29.8 us
    pallas_call x1, Pallas kernels, per_device(): pl.pallas_call(functools.partial(field_kernel, runs, chunk), out_shape=ja...  3.89 us

profile of v2, /device:TPU:0, one launch (start us, length us, event | category | flops | bytes accessed | tf_op | source)
XLA Modules:
  0.0 33.7 jit_solution(8128716202878557360)
XLA Ops:
  0.0 29.8 %rays.1 = (bf16[256,256]{1,0:T(8,128)(2,1)S(1)}, bf16[2,64,256,128]{3,2,1,0:T(8,128)(2,1)S(1)}, bf16[64,256,256]{2,1,0:T(8,128)(2,1)S(1)}) custom-call(bf16[128,256,128]{2,1,0:T(8,128)(2,1)} %cur_hbm.1, bf16[64,256,256]{2,1,0:T(8,128)(2,1)} %agg_hbm.1, bf16[64,256,256]{2,1,0:T(8,128)(2,1)} %dis_hbm.1, f32[16,64,256]{2,1,0:T(8,128)} %coef_hbm.1, ...), custom_call_target="tpu_custom_call" | custom-call | tf_op jit(solution)/shard_map/rays/pallas_call | solution.py:534
  29.8 3.9 %field.1 = bf16[2,64,256,128]{3,2,1,0:T(8,128)(2,1)} custom-call(bf16[64,256,256]{2,1,0:T(8,128)(2,1)S(1)} %get-tuple-element.8.maps_ref, bf16[256,256]{1,0:T(8,128)(2,1)S(1)} %get-tuple-element.9.incoming_ref, bf16[2,64,256,128]{3,2,1,0:T(8,128)(2,1)S(1)} %get-tuple-element.10.near_ref), custom_call_target="tpu_custom_call" | custom-call | tf_op jit(solution)/shard_map/field/pallas_call | solution.py:597

commit v3 on v2

--- a/solution.py
+++ b/solution.py
@@ -12,7 +12,7 @@
 AGG_CHUNK = 4
 NEAR_BLOCK = 8
 REACH = 2
-RELAY_FROM = 2
+EARLY_BLOCKS = 3
 
 
 def split_high_low(value):
@@ -134,8 +134,6 @@
     small = [pltpu.make_async_copy(a, b, small_sem.at[i]) for i, (a, b) in enumerate(small)]
     small[0].start()
     lax.fori_loop(0, chunks, start_loads, 0)
-    for copy in small[1:]:
-        copy.start()
 
     barrier = pltpu.get_barrier_semaphore()
     for kb, kd in peers:
@@ -177,7 +175,10 @@
         acc[...] += dot(maps, held)
         return carry
 
-    lax.fori_loop(0, chunks, aggregate, 0)
+    lax.fori_loop(0, chunks - 2, aggregate, 0)
+    for copy in small[1:]:
+        copy.start()
+    lax.fori_loop(chunks - 2, chunks, aggregate, 0)
 
     def parent_copy(kb, kd):
         tb, td = target(kb, kd)
@@ -245,10 +246,10 @@
     pl.semaphore_wait(barrier, len(peers))
     deltas = sorted(range(-REACH, REACH + 1), key=lambda delta: -abs(delta))
     deltas = [delta for delta in deltas if abs(delta) < boxes]
+    for kb, kd in peers:
+        parent_copy(kb, kd).start()
     for delta in deltas:
         when_sending(delta, lambda copy: copy.start())
-    for kb, kd in peers:
-        parent_copy(kb, kd).start()
 
     @pl.when(me < devices - 1)
     def _():
@@ -304,27 +305,34 @@
                 pl.when(fits)(functools.partial(action, side, away))
 
     blocks = leaf_top // NEAR_BLOCK
-    per_step = -(-dirs // (blocks - 2 - RELAY_FROM))
-
-    def near_step(step, carry):
-        near_block(step + 1)
-
-        @pl.when(step >= RELAY_FROM)
-        def _():
-            def forward(side, away):
-                for i in range(per_step):
-                    sd = (step - RELAY_FROM) * per_step + i
-
-                    @pl.when(sd < dirs)
-                    def _():
-                        ray_arrived(my_box - side * away, sd)
-                        relay_copy(side, away, sd).start()
-
-            each_relay(forward)
-
-        return carry
-
-    lax.fori_loop(0, blocks - 2, near_step, 0)
+    late_blocks = blocks - 2 - EARLY_BLOCKS
+    per_step = dirs // (late_blocks + 1)
+
+    def near_only(step, carry):
+        near_block(step)
+        return carry
+
+    def relay(side, away, i, carry):
+        sd = lax.rem(my_dir - i + dirs, dirs)
+        ray_arrived(my_box - side * away, sd)
+        relay_copy(side, away, sd).start()
+        return carry
+
+    def relay_span(first, last):
+        def some(side, away):
+            lax.fori_loop(first, last, functools.partial(relay, side, away), 0)
+
+        each_relay(some)
+
+    def near_relay(step, carry):
+        near_block(step)
+        first = (step - EARLY_BLOCKS - 1) * per_step
+        relay_span(first, first + per_step)
+        return carry
+
+    lax.fori_loop(1, 1 + EARLY_BLOCKS, near_only, 0)
+    lax.fori_loop(1 + EARLY_BLOCKS, blocks - 1, near_relay, 0)
+    relay_span(late_blocks * per_step, dirs)
 
     spread_time = pltpu.roll(
         jnp.broadcast_to(kernel_ref[...], (samples, samples)), 0, 1, stride=1, stride_axis=0
@@ -389,7 +397,6 @@
         return carry
 
     lax.fori_loop(0, boxes, spread, 0)
-
     half = lax.div(my_box * 2, boxes)
     for n in range(boxes):
         sb = lax.rem(my_box + n * (1 - 2 * half) + boxes, boxes)

time: 33.9 us -> 30.2 us (0.89)
  Pallas kernels: 33.7 us -> 30 us
    pallas_call x1, Pallas kernels: 29.8 us -> 26.1 us  [per_device(): pl.pallas_call(functools.partial(rays_kernel, boxes, dirs, runs), out_sha...]
where the time goes in v3:
time: 30.2 us; the launch traced here: 30 us
  Pallas kernels  30 us (99%)
    pallas_call x1, Pallas kernels, per_device(): pl.pallas_call(functools.partial(rays_kernel, boxes, dirs, runs), out_sha...  26.1 us
    pallas_call x1, Pallas kernels, per_device(): pl.pallas_call(functools.partial(field_kernel, runs, chunk), out_shape=ja...  3.89 us

profile of v3, /device:TPU:0, one launch (start us, length us, event | category | flops | bytes accessed | tf_op | source)
XLA Modules:
  0.0 30.0 jit_solution(3712966704827013501)
XLA Ops:
  0.0 26.1 %rays.1 = (bf16[256,256]{1,0:T(8,128)(2,1)S(1)}, bf16[2,64,256,128]{3,2,1,0:T(8,128)(2,1)S(1)}, bf16[64,256,256]{2,1,0:T(8,128)(2,1)S(1)}) custom-call(bf16[128,256,128]{2,1,0:T(8,128)(2,1)} %cur_hbm.1, bf16[64,256,256]{2,1,0:T(8,128)(2,1)} %agg_hbm.1, bf16[64,256,256]{2,1,0:T(8,128)(2,1)} %dis_hbm.1, f32[16,64,256]{2,1,0:T(8,128)} %coef_hbm.1, ...), custom_call_target="tpu_custom_call" | custom-call | tf_op jit(solution)/shard_map/rays/pallas_call | solution.py:541
  26.1 3.9 %field.1 = bf16[2,64,256,128]{3,2,1,0:T(8,128)(2,1)} custom-call(bf16[64,256,256]{2,1,0:T(8,128)(2,1)S(1)} %get-tuple-element.8.maps_ref, bf16[256,256]{1,0:T(8,128)(2,1)S(1)} %get-tuple-element.9.incoming_ref, bf16[2,64,256,128]{3,2,1,0:T(8,128)(2,1)S(1)} %get-tuple-element.10.near_ref), custom_call_target="tpu_custom_call" | custom-call | tf_op jit(solution)/shard_map/field/pallas_call | solution.py:604

commit v4 on v3

--- a/solution.py
+++ b/solution.py
@@ -175,11 +175,6 @@
         acc[...] += dot(maps, held)
         return carry
 
-    lax.fori_loop(0, chunks - 2, aggregate, 0)
-    for copy in small[1:]:
-        copy.start()
-    lax.fori_loop(chunks - 2, chunks, aggregate, 0)
-
     def parent_copy(kb, kd):
         tb, td = target(kb, kd)
         return pltpu.make_async_remote_copy(
@@ -190,6 +185,14 @@
             device_id={"box": tb, "dir": td},
             device_id_type=MESH,
         )
+
+    lax.fori_loop(0, chunks - 4, aggregate, 0)
+    for copy in small[1:]:
+        copy.start()
+    pl.semaphore_wait(barrier, len(peers))
+    for kb, kd in peers:
+        parent_copy(kb, kd).start()
+    lax.fori_loop(chunks - 4, chunks, aggregate, 0)
 
     def ray_copy(delta, kd):
         tb = my_box + delta
@@ -243,11 +246,8 @@
 
     for j in range(runs):
         rays[j] = acc[:, j * samples : (j + 1) * samples].astype(BF16)
-    pl.semaphore_wait(barrier, len(peers))
     deltas = sorted(range(-REACH, REACH + 1), key=lambda delta: -abs(delta))
     deltas = [delta for delta in deltas if abs(delta) < boxes]
-    for kb, kd in peers:
-        parent_copy(kb, kd).start()
     for delta in deltas:
         when_sending(delta, lambda copy: copy.start())
 
@@ -503,7 +503,7 @@
         return carry
 
     steps = leaf_top // chunk
-    lax.fori_loop(0, steps, step_of, 0, unroll=4)
+    lax.fori_loop(0, steps, step_of, 0, unroll=8)
     lax.fori_loop(0, steps, finish, 0)
 
 

time: 30.2 us -> 29.8 us (0.987)
  no operation moved by 1% of the time
where the time goes in v4:
time: 29.8 us; the launch traced here: 29.7 us
  Pallas kernels  29.7 us (100%)
    pallas_call x1, Pallas kernels, per_device(): pl.pallas_call(functools.partial(rays_kernel, boxes, dirs, runs), out_sha...  25.9 us
    pallas_call x1, Pallas kernels, per_device(): pl.pallas_call(functools.partial(field_kernel, runs, chunk), out_shape=ja...  3.74 us

profile of v4, /device:TPU:0, one launch (start us, length us, event | category | flops | bytes accessed | tf_op | source)
XLA Modules:
  0.0 29.7 jit_solution(18367677990207392988)
XLA Ops:
  0.0 25.9 %rays.1 = (bf16[256,256]{1,0:T(8,128)(2,1)S(1)}, bf16[2,64,256,128]{3,2,1,0:T(8,128)(2,1)S(1)}, bf16[64,256,256]{2,1,0:T(8,128)(2,1)S(1)}) custom-call(bf16[128,256,128]{2,1,0:T(8,128)(2,1)} %cur_hbm.1, bf16[64,256,256]{2,1,0:T(8,128)(2,1)} %agg_hbm.1, bf16[64,256,256]{2,1,0:T(8,128)(2,1)} %dis_hbm.1, f32[16,64,256]{2,1,0:T(8,128)} %coef_hbm.1, ...), custom_call_target="tpu_custom_call" | custom-call | tf_op jit(solution)/shard_map/rays/pallas_call | solution.py:541
  25.9 3.7 %field.1 = bf16[2,64,256,128]{3,2,1,0:T(8,128)(2,1)} custom-call(bf16[64,256,256]{2,1,0:T(8,128)(2,1)S(1)} %get-tuple-element.8.maps_ref, bf16[256,256]{1,0:T(8,128)(2,1)S(1)} %get-tuple-element.9.incoming_ref, bf16[2,64,256,128]{3,2,1,0:T(8,128)(2,1)S(1)} %get-tuple-element.10.near_ref), custom_call_target="tpu_custom_call" | custom-call | tf_op jit(solution)/shard_map/field/pallas_call | solution.py:604

commit v5 on v4

--- a/solution.py
+++ b/solution.py
@@ -186,13 +186,13 @@
             device_id_type=MESH,
         )
 
-    lax.fori_loop(0, chunks - 4, aggregate, 0)
+    lax.fori_loop(0, chunks - 6, aggregate, 0)
     for copy in small[1:]:
         copy.start()
     pl.semaphore_wait(barrier, len(peers))
     for kb, kd in peers:
         parent_copy(kb, kd).start()
-    lax.fori_loop(chunks - 4, chunks, aggregate, 0)
+    lax.fori_loop(chunks - 6, chunks, aggregate, 0)
 
     def ray_copy(delta, kd):
         tb = my_box + delta

time: 29.8 us -> 29.8 us (level)
  no operation moved by 1% of the time
where the time goes in v5:
time: 29.8 us; the launch traced here: 29.6 us
  Pallas kernels  29.6 us (99%)
    pallas_call x1, Pallas kernels, per_device(): pl.pallas_call(functools.partial(rays_kernel, boxes, dirs, runs), out_sha...  25.9 us
    pallas_call x1, Pallas kernels, per_device(): pl.pallas_call(functools.partial(field_kernel, runs, chunk), out_shape=ja...  3.74 us

profile of v5, /device:TPU:0, one launch (start us, length us, event | category | flops | bytes accessed | tf_op | source)
XLA Modules:
  0.0 29.6 jit_solution(17787251701242682251)
XLA Ops:
  0.0 25.9 %rays.1 = (bf16[256,256]{1,0:T(8,128)(2,1)S(1)}, bf16[2,64,256,128]{3,2,1,0:T(8,128)(2,1)S(1)}, bf16[64,256,256]{2,1,0:T(8,128)(2,1)S(1)}) custom-call(bf16[128,256,128]{2,1,0:T(8,128)(2,1)} %cur_hbm.1, bf16[64,256,256]{2,1,0:T(8,128)(2,1)} %agg_hbm.1, bf16[64,256,256]{2,1,0:T(8,128)(2,1)} %dis_hbm.1, f32[16,64,256]{2,1,0:T(8,128)} %coef_hbm.1, ...), custom_call_target="tpu_custom_call" | custom-call | tf_op jit(solution)/shard_map/rays/pallas_call | solution.py:541
  25.9 3.7 %field.1 = bf16[2,64,256,128]{3,2,1,0:T(8,128)(2,1)} custom-call(bf16[64,256,256]{2,1,0:T(8,128)(2,1)S(1)} %get-tuple-element.8.maps_ref, bf16[256,256]{1,0:T(8,128)(2,1)S(1)} %get-tuple-element.9.incoming_ref, bf16[2,64,256,128]{3,2,1,0:T(8,128)(2,1)S(1)} %get-tuple-element.10.near_ref), custom_call_target="tpu_custom_call" | custom-call | tf_op jit(solution)/shard_map/field/pallas_call | solution.py:604

commit v6 on v5

--- a/solution.py
+++ b/solution.py
@@ -503,7 +503,7 @@
         return carry
 
     steps = leaf_top // chunk
-    lax.fori_loop(0, steps, step_of, 0, unroll=8)
+    lax.fori_loop(0, steps, step_of, 0, unroll=16)
     lax.fori_loop(0, steps, finish, 0)
 
 
@@ -599,7 +599,7 @@
         held(time_kernel.reshape(1, samples)),
     )
 
-    chunk = 4
+    chunk = 2
     out_shape = (runs, leaf_top, unknowns, samples)
     out = pl.pallas_call(
         functools.partial(field_kernel, runs, chunk),

time: 29.8 us -> 29.8 us (level)
  no operation moved by 1% of the time
where the time goes in v6:
time: 29.8 us; the launch traced here: 29.7 us
  Pallas kernels  29.7 us (100%)
    pallas_call x1, Pallas kernels, per_device(): pl.pallas_call(functools.partial(rays_kernel, boxes, dirs, runs), out_sha...  25.9 us
    pallas_call x1, Pallas kernels, per_device(): pl.pallas_call(functools.partial(field_kernel, runs, chunk), out_shape=ja...  3.79 us

profile of v6, /device:TPU:0, one launch (start us, length us, event | category | flops | bytes accessed | tf_op | source)
XLA Modules:
  0.0 29.7 jit_solution(3646191335264215352)
XLA Ops:
  0.0 25.9 %rays.1 = (bf16[256,256]{1,0:T(8,128)(2,1)S(1)}, bf16[2,64,256,128]{3,2,1,0:T(8,128)(2,1)S(1)}, bf16[64,256,256]{2,1,0:T(8,128)(2,1)S(1)}) custom-call(bf16[128,256,128]{2,1,0:T(8,128)(2,1)} %cur_hbm.1, bf16[64,256,256]{2,1,0:T(8,128)(2,1)} %agg_hbm.1, bf16[64,256,256]{2,1,0:T(8,128)(2,1)} %dis_hbm.1, f32[16,64,256]{2,1,0:T(8,128)} %coef_hbm.1, ...), custom_call_target="tpu_custom_call" | custom-call | tf_op jit(solution)/shard_map/rays/pallas_call | solution.py:541
  25.9 3.8 %field.1 = bf16[2,64,256,128]{3,2,1,0:T(8,128)(2,1)} custom-call(bf16[64,256,256]{2,1,0:T(8,128)(2,1)S(1)} %get-tuple-element.8.maps_ref, bf16[256,256]{1,0:T(8,128)(2,1)S(1)} %get-tuple-element.9.incoming_ref, bf16[2,64,256,128]{3,2,1,0:T(8,128)(2,1)S(1)} %get-tuple-element.10.near_ref), custom_call_target="tpu_custom_call" | custom-call | tf_op jit(solution)/shard_map/field/pallas_call | solution.py:604
